TPU v7x, 128 devices: a whole 4x4x4 slice. The times are simulated.
128 devices in a mesh: gx: 4 (over y), gy: 4 (over x_hi, core), gz: 8 (over z, x_lo).
Axes of the slice: x: 4 (x_hi: 2, x_lo: 2; x = x_hi * 2 + x_lo), y: 4, z: 4, core: 2. Of those that a mesh axis runs over, the one named last changes fastest.
Arguments:
- concentration: float32 [512, 512, 512], P('gz', 'gx', 'gy'), may hold values from -1 to 1
Outputs:
- concentration_next: float32 [512, 512, 512], P('gz', 'gx', 'gy')
All inputs are finite; a program needn't handle non-finite values.
Results may differ from a plain program's by a relative error of at most 0.00011.
Values sent between devices are 32-bit elements; how exact they have to be, the bound alone decides.
A program may use at most 192 MiB of HBM per device.

v0:
```python
import functools

import jax
import jax.numpy as jnp
from jax import lax
from jax.sharding import Mesh
from jax.sharding import PartitionSpec as P

GY = ("gy_0", "gy_1")
GZ = ("gz_0", "gz_1")
GX_GY_GZ = ("gx", "gy_0", "gy_1", "gz_0", "gz_1")


step_length = 0.2
stiffness = 0.25


def padded_2(x, sides, width):
    edges = {}
    for axis, dim in sides:
        count, length = (lax.axis_size(axis), x.shape[dim])
        up = [(i, (i + 1) % count) for i in range(count)]
        last = lax.slice_in_dim(x, length - width, length, axis=dim)
        leading = lax.slice_in_dim(x, 0, width, axis=dim)
        edges[dim] = (
            lax.ppermute(last, axis, up),
            lax.ppermute(leading, axis, [(b, a) for a, b in up]),
        )
    done = []
    for _, dim in sides:
        low, high = edges[dim]
        around = [(width, width) if d in done else (0, 0) for d in range(x.ndim)]
        x = jnp.concatenate([jnp.pad(low, around), x, jnp.pad(high, around)], axis=dim)
        done.append(dim)
    return x


def by_axis(x, axes):
    return functools.reduce(lax.psum, axes, x)


def hartley_table(length):
    indices = jnp.arange(length, dtype=jnp.int32)
    product = indices[:, None] * indices[None, :] % length
    angles = 2.0 * jnp.pi / length * product.astype(jnp.float32)
    return (jnp.cos(angles) + jnp.sin(angles)) / jnp.sqrt(float(length))


def wave_square(length):
    indices = jnp.arange(length, dtype=jnp.int32)
    folded = jnp.minimum(indices, length - indices).astype(jnp.float32)
    wave = 2.0 * jnp.pi / length * folded
    return wave * wave


def column_matmul(matrix, source):
    flat_columns = source.reshape(source.shape[0], -1)
    mapped = jnp.dot(
        matrix, flat_columns, precision=lax.Precision.HIGHEST, preferred_element_type=jnp.float32
    )
    return mapped.reshape(source.shape)


def plane_pass(planes, hartley_x, hartley_y):
    mapped = jnp.einsum("ij,rjy->riy", hartley_x, planes, precision=lax.Precision.HIGHEST)
    flat_planes = mapped.reshape(-1, planes.shape[2])
    mapped = jnp.dot(
        flat_planes,
        hartley_y.T,
        precision=lax.Precision.HIGHEST,
        preferred_element_type=jnp.float32,
    )
    return mapped.reshape(planes.shape)


def face_terms(padded_pot, padded_mob, axis_number):
    length = padded_pot.shape[axis_number]
    lower_pot = lax.slice_in_dim(padded_pot, 0, length - 1, axis=axis_number)
    upper_pot = lax.slice_in_dim(padded_pot, 1, length, axis=axis_number)
    lower_mob = lax.slice_in_dim(padded_mob, 0, length - 1, axis=axis_number)
    upper_mob = lax.slice_in_dim(padded_mob, 1, length, axis=axis_number)
    flux = 0.5 * (lower_mob + upper_mob) * (upper_pot - lower_pot)
    count = flux.shape[axis_number]
    return lax.slice_in_dim(flux, 1, count, axis=axis_number) - lax.slice_in_dim(
        flux, 0, count - 1, axis=axis_number
    )


def solve_planes(planes, hartley_x, hartley_y, local_z, wave_x, wave_y, mean_mobility):
    planes = plane_pass(planes, hartley_x, hartley_y)
    wave_sum = local_z[:, None, None] + wave_x[None, :, None] + wave_y[None, None, :]
    planes = planes / (1.0 + step_length * stiffness * mean_mobility * wave_sum * wave_sum)
    return plane_pass(planes, hartley_x, hartley_y)


def local(concentration):
    block_z, block_x, block_y = concentration.shape
    groups_x = lax.axis_size("gx")
    groups_y = lax.axis_size(GY)
    groups_z = lax.axis_size(GZ)
    whole_z = block_z * groups_z
    whole_x = block_x * groups_x
    whole_y = block_y * groups_y
    hartley_z = hartley_table(whole_z)
    hartley_x = hartley_table(whole_x)
    hartley_y = hartley_table(whole_y)
    padded = padded_2(concentration, (("gx", 1), (GY, 2), (GZ, 0)), 1)
    padded_pot = padded * padded * padded - padded
    padded_mob = 1.05 - padded * padded
    mobility = padded_mob[1:-1, 1:-1, 1:-1]
    mobility_sum = by_axis(jnp.sum(mobility), GX_GY_GZ)
    mean_mobility = mobility_sum / (whole_x * whole_y * whole_z)
    divergence = face_terms(padded_pot[:, 1:-1, 1:-1], padded_mob[:, 1:-1, 1:-1], 0)
    divergence = divergence + face_terms(padded_pot[1:-1, :, 1:-1], padded_mob[1:-1, :, 1:-1], 1)
    divergence = divergence + face_terms(padded_pot[1:-1, 1:-1, :], padded_mob[1:-1, 1:-1, :], 2)
    update = concentration + step_length * divergence
    wave_z = wave_square(whole_z)
    wave_x = wave_square(whole_x)
    wave_y = wave_square(whole_y)
    devices = groups_x * groups_y * groups_z
    rows_each = whole_z // devices
    slim_x = block_x // groups_z
    member = (lax.axis_index("gx") * groups_y + lax.axis_index(GY)) * groups_z + lax.axis_index(GZ)
    pencil = lax.all_to_all(update, GZ, split_axis=1, concat_axis=0, tiled=True)
    pencil = column_matmul(hartley_z, pencil)
    outgoing = pencil.reshape(devices, rows_each, slim_x, block_y)
    received = lax.all_to_all(outgoing, GX_GY_GZ, split_axis=0, concat_axis=0, tiled=True)
    planes = received.reshape(groups_x, groups_y, groups_z, rows_each, slim_x, block_y)
    planes = planes.transpose(3, 0, 2, 4, 1, 5).reshape(rows_each, whole_x, whole_y)
    local_z = lax.dynamic_slice_in_dim(wave_z, member * rows_each, rows_each, 0)
    planes = solve_planes(planes, hartley_x, hartley_y, local_z, wave_x, wave_y, mean_mobility)
    returning = planes.reshape(rows_each, groups_x, groups_z, slim_x, groups_y, block_y)
    returning = returning.transpose(1, 4, 2, 0, 3, 5).reshape(devices, rows_each, slim_x, block_y)
    arrived = lax.all_to_all(returning, GX_GY_GZ, split_axis=0, concat_axis=0, tiled=True)
    pencil = column_matmul(hartley_z, arrived.reshape(whole_z, slim_x, block_y))
    return lax.all_to_all(pencil, GZ, split_axis=0, concat_axis=1, tiled=True)


def solution(mesh):
    torus = Mesh(
        mesh.devices.reshape(mesh.shape["gx"], 2, 2, 4, 2), ("gx", "gy_0", "gy_1", "gz_0", "gz_1")
    )
    in_specs = (P(GZ, "gx", GY),)
    out_specs = P(GZ, "gx", GY)
    return jax.shard_map(local, mesh=torus, in_specs=in_specs, out_specs=out_specs, check_vma=False)
```

profile of v0, /device:TPU:1, one launch (start us, length us, event | category | flops | bytes accessed | tf_op | source)
XLA Modules:
  0.0 494.6 jit_solution(6628184515026197495)
XLA Ops:
  0.0 8.1 %fusion.113 = (f32[64,128,1]{2,1,0:T(8,128)}, f32[64,128,1]{2,1,0:T(8,128)}) fusion(f32[64,128,128]{2,1,0:T(8,128)} %param.1), kind=kLoop, calls=%fused_computation.146 | loop fusion | bytes 131072 | tf_op jit(solution)/shard_map/slice | solution.py:23
  41.6 12.8 %multiply_subtract_fusion.1 = (f32[66,130,130]{2,0,1:T(8,128)S(1)}, f32[66,130,130]{2,0,1:T(8,128)}) fusion(f32[1,128,128]{2,0,1:T(1,128)S(1)} %collective-permute-done.5, f32[64,128,1]{2,0,1:T(8,128)} %copy.38, f32[64,1,128]{2,0,1:T(8,128)S(1)} %collective-permute-done.3, f32[64,128,128]{2,0,1:T(8,128)} %copy-done.1, ...), kind=kLoop, calls=%fused_computation.3 | loop fusion | flops 27885000 | bytes 13379648 | tf_op jit(solution)/shard_map/sub | solution.py:109
  54.3 14.1 %fusion.6 = f32[65,128,128]{2,0,1:T(8,128)} fusion(f32[66,130,130]{2,0,1:T(8,128)} %get-tuple-element.6, f32[66,130,130]{2,0,1:T(8,128)S(1)} %get-tuple-element.5), kind=kLoop, calls=%fused_computation.21 | loop fusion | flops 4259840 | bytes 21299200 | tf_op jit(solution)/shard_map/mul | solution.py:82
  68.5 10.4 %fusion.8 = f32[64,129,128]{2,0,1:T(8,128)} fusion(f32[66,130,130]{2,0,1:T(8,128)} %get-tuple-element.6, f32[66,130,130]{2,0,1:T(8,128)S(1)} %get-tuple-element.5), kind=kLoop, calls=%fused_computation.25 | loop fusion | flops 4227072 | bytes 21135360 | tf_op jit(solution)/shard_map/mul | solution.py:82
  78.8 15.2 %fusion.4 = f32[64,128,129]{2,0,1:T(8,128)} fusion(f32[66,130,130]{2,0,1:T(8,128)} %get-tuple-element.6, f32[66,130,130]{2,0,1:T(8,128)S(1)} %get-tuple-element.5), kind=kLoop, calls=%fused_computation.16 | loop fusion | flops 4227072 | bytes 21135360 | tf_op jit(solution)/shard_map/mul | solution.py:82
  94.1 14.9 %fusion.16 = f32[64,128,128]{2,0,1:T(8,128)} fusion(f32[64,128,129]{2,0,1:T(8,128)} %fusion.4, f32[64,129,128]{2,0,1:T(8,128)} %fusion.8, f32[65,128,128]{2,0,1:T(8,128)} %fusion.6, f32[64,128,128]{2,1,0:T(8,128)} %param.1), kind=kLoop, calls=%fused_computation.37 | loop fusion | flops 7340032 | bytes 33554432 | tf_op jit(solution)/shard_map/add | solution.py:116
  113.6 47.3 %all-to-all-done = f32[64,128,128]{2,0,1:T(8,128)} async-done(((f32[64,128,128]{2,0,1:T(8,128)}), f32[64,128,128]{2,0,1:T(8,128)}, u32[]{:S(2)}, u32[]{:S(2)}) %all-to-all-start) | async-done | bytes 4194336 | tf_op jit(solution)/shard_map/all_to_all | solution.py:124
  169.4 5.8 %copy.21 = f32[2048,512]{1,0:T(8,128)} copy(f32[2048,512]{0,1:T(8,128)} %bitcast.74) | data formatting | bytes 8388608 | tf_op jit(solution)/shard_map/dot_general | solution.py:58
  175.2 13.2 %fusion.35 = f32[128,4,16,128]{3,0,2,1:T(8,128)S(1)} fusion(f32[16,128,512,1]{2,1,0,3:T(8,128)} %bitcast.72, s32[128,4]{0,1:T(4,128)S(1)} %multiply_add_fusion.1), kind=kOutput, calls=%fused_computation.69 | convolution fusion | flops 6446645248 | bytes 8390656 | tf_op jit(solution)/shard_map/dot_general | solution.py:58
  193.0 8.7 %all-to-all-start.1 = ((f32[128,4,16,128]{3,2,1,0:T(8,128)}), f32[128,4,16,128]{3,2,1,0:T(8,128)}, u32[]{:S(2)}, u32[]{:S(2)}) async-start(f32[128,4,16,128]{3,2,1,0:T(8,128)} %copy.22), calls=%async_computation.1 | async-start | bytes 8388608 | tf_op jit(solution)/shard_map/all_to_all | solution.py:127
  207.2 41.8 %psum.35 = f32[]{:T(128)} all-reduce(f32[]{:T(128)} %slice_reduce_fusion), channel_id=1, replica_groups=mesh['gx'=4,'gy_0'=2,'gy_1'=2,'gz_0'=4,'gz_1'=2] {'gx'}, use_global_device_ids=true, to_apply=%region_1.2 | all-reduce | flops 1 | bytes 8 | tf_op jit(solution)/shard_map/psum | solution.py:39
  249.0 7.2 %psum.36 = f32[]{:T(128)} all-reduce(f32[]{:T(128)} %psum.35), channel_id=1, replica_groups=mesh['gx'=4,'gy_0'=2,'gy_1'=2,'gz_0'=4,'gz_1'=2] {'gy_0'}, use_global_device_ids=true, to_apply=%region_2.3 | all-reduce | flops 1 | bytes 8 | tf_op jit(solution)/shard_map/psum | solution.py:39
  256.2 5.5 %psum.37 = f32[]{:T(128)} all-reduce(f32[]{:T(128)} %psum.36), channel_id=1, replica_groups=mesh['gx'=4,'gy_0'=2,'gy_1'=2,'gz_0'=4,'gz_1'=2] {'gy_1'}, use_global_device_ids=true, to_apply=%region_3.4 | all-reduce | flops 1 | bytes 8 | tf_op jit(solution)/shard_map/psum | solution.py:39
  261.8 10.4 %psum.38 = f32[]{:T(128)} all-reduce(f32[]{:T(128)} %psum.37), channel_id=1, replica_groups=mesh['gx'=4,'gy_0'=2,'gy_1'=2,'gz_0'=4,'gz_1'=2] {'gz_0'}, use_global_device_ids=true, to_apply=%region_4.5 | all-reduce | flops 1 | bytes 8 | tf_op jit(solution)/shard_map/psum | solution.py:39
  277.2 6.9 %copy.47 = f32[4,4,8,4,16,128]{5,1,4,2,0,3:T(4,128)} copy(f32[4,4,8,4,16,128]{5,4,3,2,1,0:T(8,128)} %bitcast.11) | data formatting | bytes 8388608 | tf_op jit(solution)/shard_map/reshape | solution.py:128
  284.1 5.5 %reshape.232 = f32[4,512,512]{2,1,0:T(8,128)} reshape(f32[4,4,8,16,4,128]{5,4,3,2,1,0:T(4,128)} %bitcast.75) | data formatting | bytes 8388608 | tf_op jit(solution)/shard_map/reshape | solution.py:129
  289.6 20.3 %fusion.41 = f32[4,512,512]{2,1,0:T(8,128)S(1)} fusion(f32[4,512,512]{2,1,0:T(8,128)} %reshape.232), kind=kOutput, calls=%fused_computation.75 | convolution fusion | flops 6446645248 | bytes 8388608 | tf_op jit(solution)/shard_map/ij,rjy->riy/dot_general | solution.py:65
  309.8 19.9 %fusion.18 = f32[4,512,512]{2,1,0:T(8,128)S(1)} fusion(f32[4,512,512]{2,1,0:T(8,128)S(1)} %fusion.41), kind=kOutput, calls=%fused_computation.41 | convolution fusion | flops 6446645248 | bytes 8388608 | tf_op jit(solution)/shard_map/dot_general | solution.py:67
  329.7 13.4 %fusion.12 = f32[4,512,512]{1,2,0:T(8,128)S(1)} fusion(f32[4,512,512]{2,1,0:T(8,128)S(1)} %fusion.18, f32[512]{0:T(512)S(1)} %fusion.80, f32[4,512]{1,0:T(4,128)S(1)} %broadcast_add_fusion, f32[]{:T(128)S(6)} %mul_shard_map.3), kind=kOutput, calls=%fused_computation.30 | convolution fusion | flops 6451888128 | bytes 8398852 | tf_op jit(solution)/shard_map/ij,rjy->riy/dot_general | solution.py:65
  343.2 11.1 %convolution_bitcast_fusion = f32[4,4,8,4,16,128]{5,4,1,2,0,3:T(8,128)S(1)} fusion(f32[4,4,8,16,512,1]{4,3,5,2,1,0:T(8,128)S(1)} %bitcast.80, s32[4,128]{1,0:T(4,128)S(1)} %multiply_add_fusion), kind=kOutput, calls=%fused_computation.45 | convolution fusion | flops 6446645248 | bytes 8390656 | tf_op jit(solution)/shard_map/dot_general | solution.py:67
  354.9 61.5 %all_to_all.43 = f32[128,4,16,128]{3,2,1,0:T(8,128)S(1)} all-to-all(f32[128,4,16,128]{3,2,1,0:T(8,128)S(1)} %bitcast.76), channel_id=1, replica_groups=mesh['gx'=4,'gy_0'=2,'gy_1'=2,'gz_0'=4,'gz_1'=2] {'gx','gy_0','gy_1','gz..., dimensions={0} | all-to-all | bytes 8388608 | tf_op jit(solution)/shard_map/all_to_all | solution.py:134
  420.3 5.5 %copy.27 = f32[2048,512]{1,0:T(8,128)} copy(f32[2048,512]{0,1:T(8,128)} %bitcast.78) | data formatting | bytes 8388608 | tf_op jit(solution)/shard_map/dot_general | solution.py:58
  425.8 13.2 %fusion.37 = f32[512,16,128]{2,0,1:T(8,128)S(1)} fusion(f32[16,128,512]{2,1,0:T(8,128)} %bitcast.71), kind=kOutput, calls=%fused_computation.71 | convolution fusion | flops 6446645248 | bytes 8388608 | tf_op jit(solution)/shard_map/dot_general | solution.py:58
  441.4 50.3 %all_to_all.44 = f32[512,16,128]{2,1,0:T(8,128)S(1)} all-to-all(f32[512,16,128]{2,1,0:T(8,128)S(1)} %copy.28), channel_id=1, replica_groups=mesh['gx'=4,'gy_0'=2,'gy_1'=2,'gz_0'=4,'gz_1'=2] {'gz_0','gz_1'}, dimensions={0} | all-to-all | bytes 8388608 | tf_op jit(solution)/shard_map/all_to_all | solution.py:136
  (39 shorter events, 70.8 us)
Async XLA Ops:
  10.9 19.8 %collective-permute-start.1 = (f32[64,128,1]{1,0,2:T(8,128)S(1)}, f32[64,128,1]{1,0,2:T(8,128)S(1)}, u32[]{:S(2)}, u32[]{:S(2)}) collective-permute-start(f32[64,128,1]{1,0,2:T(8,128)S(1)} %copy.35), channel_id=1, source_target_pairs={{0,8},{8,16},{16,24},{24,0},{1,9},{9,17},{17,25},{25,1},{2,10},{10... | collective-permute-start | bytes 98312 | tf_op jit(solution)/shard_map/ppermute | solution.py:26
  16.0 25.5 %collective-permute-start = (f32[1,128,128]{2,0,1:T(1,128)S(1)}, f32[1,128,128]{2,0,1:T(1,128)S(1)}, u32[]{:S(2)}, u32[]{:S(2)}) collective-permute-start(f32[1,128,128]{2,0,1:T(1,128)S(1)} %bitcast.82), channel_id=1, source_target_pairs={{0,1},{1,2},{2,3},{3,4},{4,5},{5,6},{6,7},{7,0},{8,9},{9,10},{10,1... | collective-permute-start | bytes 196616 | tf_op jit(solution)/shard_map/ppermute | solution.py:26
  16.4 25.2 %collective-permute-start.5 = (f32[1,128,128]{2,0,1:T(1,128)S(1)}, f32[1,128,128]{2,0,1:T(1,128)S(1)}, u32[]{:S(2)}, u32[]{:S(2)}) collective-permute-start(f32[1,128,128]{2,0,1:T(1,128)S(1)} %bitcast.81), channel_id=1, source_target_pairs={{1,0},{2,1},{3,2},{4,3},{5,4},{6,5},{7,6},{0,7},{9,8},{10,9},{11,1... | collective-permute-start | bytes 196616 | tf_op jit(solution)/shard_map/ppermute | solution.py:27
  24.6 1.9 copy-start.1
  26.5 15.0 %collective-permute-start.2 = (f32[64,1,128]{2,0,1:T(8,128)S(1)}, f32[64,1,128]{2,0,1:T(8,128)S(1)}, u32[]{:S(2)}, u32[]{:S(2)}) collective-permute-start(f32[64,1,128]{2,0,1:T(8,128)S(1)} %get-tuple-element.11), channel_id=1, source_target_pairs={{0,32},{32,64},{64,96},{96,0},{1,33},{33,65},{65,97},{97,1},{2,34}... | collective-permute-start | bytes 98312 | tf_op jit(solution)/shard_map/ppermute | solution.py:26
  30.6 6.5 %collective-permute-start.4 = (f32[64,128,1]{1,0,2:T(8,128)S(1)}, f32[64,128,1]{1,0,2:T(8,128)S(1)}, u32[]{:S(2)}, u32[]{:S(2)}) collective-permute-start(f32[64,128,1]{1,0,2:T(8,128)S(1)} %copy.36), channel_id=1, source_target_pairs={{8,0},{16,8},{24,16},{0,24},{9,1},{17,9},{25,17},{1,25},{10,2},{18... | collective-permute-start | bytes 98312 | tf_op jit(solution)/shard_map/ppermute | solution.py:27
  30.7 10.8 %collective-permute-start.3 = (f32[64,1,128]{2,0,1:T(8,128)S(1)}, f32[64,1,128]{2,0,1:T(8,128)S(1)}, u32[]{:S(2)}, u32[]{:S(2)}) collective-permute-start(f32[64,1,128]{2,0,1:T(8,128)S(1)} %get-tuple-element.12), channel_id=1, source_target_pairs={{32,0},{64,32},{96,64},{0,96},{33,1},{65,33},{97,65},{1,97},{34,2}... | collective-permute-start | bytes 98312 | tf_op jit(solution)/shard_map/ppermute | solution.py:27
  54.3 24.5 %copy-start = (f32[66,130,130]{2,0,1:T(8,128)}, f32[66,130,130]{2,0,1:T(8,128)S(1)}, u32[]{:S(2)}) copy-start(f32[66,130,130]{2,0,1:T(8,128)S(1)} %get-tuple-element.5) | copy-start | bytes 13384804
  109.0 51.8 %all-to-all-start = ((f32[64,128,128]{2,0,1:T(8,128)}), f32[64,128,128]{2,0,1:T(8,128)}, u32[]{:S(2)}, u32[]{:S(2)}) async-start(f32[64,128,128]{2,0,1:T(8,128)} %fusion.16), calls=%async_computation | async-start | bytes 8388608 | tf_op jit(solution)/shard_map/all_to_all | solution.py:124
  193.0 84.2 %all-to-all-start.1 = ((f32[128,4,16,128]{3,2,1,0:T(8,128)}), f32[128,4,16,128]{3,2,1,0:T(8,128)}, u32[]{:S(2)}, u32[]{:S(2)}) async-start(f32[128,4,16,128]{3,2,1,0:T(8,128)} %copy.22), calls=%async_computation.1 | async-start | bytes 8388608 | tf_op jit(solution)/shard_map/all_to_all | solution.py:127
where the time goes:
time: 502 us; the launch traced here: 495 us
  blocking collectives  181 us (36%)
  matrix products  91 us (18%)
  local copies, waits for them, and re-layouts  76.6 us (15%)
  other arithmetic  73 us (15%)
  waiting for transfers between devices  47.3 us (9%)
  starting transfers between devices  24.8 us (5%)
    psum x5, blocking collectives, by_axis(): return functools.reduce(lax.psum, axes, x)  69.3 us
    all_to_all x1, blocking collectives, local(): lax.all_to_all(returning, GX_GY_GZ, split_axis=0, concat_axis=0, tiled=True)  61.5 us
    all_to_all x1, blocking collectives, local(): return lax.all_to_all(pencil, GZ, split_axis=0, concat_axis=1, tiled=True)  50.3 us
    all_to_all x1, waiting for transfers between devices, local(): pencil = lax.all_to_all(update, GZ, split_axis=1, concat_axis=0, tiled=True)  47.3 us
    mul x3, other arithmetic, face_terms(): flux = 0.5 * (lower_mob + upper_mob) * (upper_pot - lower_pot)  39.7 us
    dot_general x2, matrix products, plane_pass(): jnp.einsum('ij,rjy->riy', hartley_x, planes, precision=lax.Precision.HIGH...  33.7 us
    dot_general x2, matrix products, plane_pass(): jnp.dot(flat_planes, hartley_y.T, precision=lax.Precision.HIGHEST, prefer...  31 us
    unnamed x11, local copies, waits for them, and re-layouts  29 us
  transfers between devices with their start and end apart: 8, of which 1 were waited for; matrix products, arithmetic and copies ran while one was open for 5% of the time, Pallas kernels for 0%

commit v1 on v0

v1 whole, which is shorter than its diff:
```python
import functools

import jax
import jax.numpy as jnp
import numpy as np
from jax import lax
from jax.experimental import pallas as pl
from jax.experimental.pallas import tpu as pltpu
from jax.sharding import PartitionSpec as P

MESH = pl.DeviceIdType.MESH
F32, BF16 = jnp.float32, jnp.bfloat16

step_length = 0.2
stiffness = 0.25

N = 512
HALF = N // 2
BZ, BX, BY = 64, 128, 128
CHUNK = 16
Z_OFFSETS = ((1, 0), (0, 1), (3, 0), (2, 0), (1, 1), (3, 1), (2, 1))


def split_table(matrix):
    high = matrix.astype(np.float32).astype(jnp.bfloat16)
    low = (matrix - high.astype(np.float64)).astype(np.float32).astype(jnp.bfloat16)
    return high, low


def tables():
    index = np.arange(N)
    angle = 2.0 * np.pi / N * (index[:, None] * index[None, :] % N)
    hartley = (np.cos(angle) + np.sin(angle)) / np.sqrt(N)
    even, odd = hartley[0::2, :HALF], hartley[1::2, :HALF]
    left, right = [], []
    for matrix in (even, odd, odd.T):
        high, low = split_table(matrix)
        left.append(np.concatenate([high, low, high], axis=1))
    for matrix in (even, odd.T, odd):
        high, low = split_table(matrix)
        right.append(np.concatenate([high, low, high], axis=0))
    return np.stack(left), np.stack(right)


def thirds(a, axis):
    high = a.astype(BF16)
    low = (a - high.astype(F32)).astype(BF16)
    return jnp.concatenate([high, high, low], axis=axis)


def matmul(a, b):
    return jnp.dot(a, b, preferred_element_type=F32)


def wave_of(position):
    true = jnp.where(position < HALF, 2 * position, 2 * position - (N - 1))
    folded = jnp.minimum(true, N - true).astype(F32)
    wave = (2.0 * np.pi / N) * folded
    return wave * wave


def iota(shape, dim):
    return lax.broadcasted_iota(jnp.int32, shape, dim)


def kernel(
    c_ref,
    left_hbm,
    right_hbm,
    o_ref,
    cz,
    xs,
    xr,
    ye,
    yr,
    yc,
    up,
    r1,
    z1,
    a2,
    pb,
    a3,
    a4,
    z4,
    work,
    waves,
    left,
    right,
    ms,
    mb,
    local_sem,
    table_sem,
    halo_send,
    halo_recv,
    p1_send,
    p1_recv,
    p2a_send,
    p2a_recv,
    p2b_send,
    p2b_recv,
    p3b_send,
    p3b_recv,
    p3a_send,
    p3a_recv,
    p4_send,
    p4_recv,
    m_send,
    m_recv,
):
    gx, gy, gz = lax.axis_index("gx"), lax.axis_index("gy"), lax.axis_index("gz")
    z_chip, x_low = gz // 2, gz % 2
    x_chip, core = (gy // 2) * 2 + x_low, gy % 2
    mine = gy * 8 + gz

    def z_peer(offset):
        dz, dx = offset
        return ((z_chip + dz) % 4) * 2 + (x_low + dx) % 2

    def plane_peer(s):
        k = s % 16
        dx = k % 4
        dz = (k // 4 + dx) % 4
        px, pz, pc = (x_chip + dx) % 4, (z_chip + dz) % 4, (core + s // 16) % 2
        return (px // 2) * 2 + pc, pz * 2 + px % 2

    def remote(src, dst, send, recv, **where):
        return pltpu.make_async_remote_copy(
            src, dst, send, recv, device_id=where, device_id_type=MESH
        )

    def drain(ref, sem):
        pltpu.make_async_copy(ref, ref, sem).wait()

    load = pltpu.make_async_copy(c_ref, cz.at[pl.ds(1, BZ)], local_sem)
    load.start()
    load_left = pltpu.make_async_copy(left_hbm, left, table_sem.at[0])
    load_right = pltpu.make_async_copy(right_hbm, right, table_sem.at[1])
    load_left.start()
    load_right.start()
    barrier = pltpu.get_barrier_semaphore()

    def greet(s, carry):
        a, b = plane_peer(s)
        pl.semaphore_signal(
            barrier, inc=1, device_id={"gy": a, "gz": b}, device_id_type=MESH
        )
        return carry

    lax.fori_loop(1, 32, greet, 0)
    for s in (1, 2, 3):
        pl.semaphore_signal(
            barrier, inc=1, device_id={"gx": (gx + s) % 4}, device_id_type=MESH
        )
    load.wait()

    flat = cz.reshape((BZ + 2) * BX, BY)
    xs[0] = flat[pl.ds(BX, BZ, stride=BX), :]
    xs[1] = flat[pl.ds(BX + BX - 1, BZ, stride=BX), :]
    lane = iota((BX, BY), 1)

    def pack(z, acc):
        turned = pltpu.roll(cz[z + 1], 2 * z, 1)
        keep = (lane == 2 * z) | (lane == (2 * z + BY - 1) % BY)
        return jnp.where(keep, turned, acc)

    ye[...] = lax.fori_loop(0, BZ, pack, jnp.zeros((BX, BY), F32))

    pl.semaphore_wait(barrier, 34)
    halo = [
        remote(c_ref.at[pl.ds(BZ - 1, 1)], cz.at[pl.ds(0, 1)], halo_send.at[0], halo_recv.at[0], gz=(gz + 1) % 8),
        remote(c_ref.at[pl.ds(0, 1)], cz.at[pl.ds(BZ + 1, 1)], halo_send.at[1], halo_recv.at[1], gz=(gz + 7) % 8),
        remote(xs.at[1], xr.at[0], halo_send.at[2], halo_recv.at[2], gx=(gx + 1) % 4),
        remote(xs.at[0], xr.at[1], halo_send.at[3], halo_recv.at[3], gx=(gx + 3) % 4),
        remote(ye, yr.at[0], halo_send.at[4], halo_recv.at[4], gy=(gy + 1) % 4),
        remote(ye, yr.at[1], halo_send.at[5], halo_recv.at[5], gy=(gy + 3) % 4),
    ]
    for copy in halo:
        copy.start()
    for copy in halo:
        copy.wait()
    yc[...] = jnp.where(lane % 2 == 0, pltpu.roll(yr[0], 1, 1), pltpu.roll(yr[1], BY - 1, 1))

    row = iota((BX, BY), 0)

    def terms(c):
        square = c * c
        return square * c - c, 1.05 - square

    def stencil(z, total):
        c = cz[z + 1]
        p, m = terms(c)
        pz, mz = terms(cz[z + 2])
        divergence = (m + mz) * (pz - p)
        pz, mz = terms(cz[z])
        divergence = divergence - (m + mz) * (p - pz)
        ph, mh = terms(jnp.broadcast_to(xr[0, pl.ds(z, 1), :], (BX, BY)))
        pp = jnp.where(row == 0, ph, pltpu.roll(p, 1, 0))
        mp = jnp.where(row == 0, mh, pltpu.roll(m, 1, 0))
        flux = (m + mp) * (p - pp)
        ph, mh = terms(jnp.broadcast_to(xr[1, pl.ds(z, 1), :], (BX, BY)))
        after = jnp.where(row == BX - 1, (m + mh) * (ph - p), pltpu.roll(flux, BX - 1, 0))
        divergence = divergence + (after - flux)
        ph, mh = terms(pltpu.roll(yc[...], (BY - 2 * z) % BY, 1))
        pp = jnp.where(lane == 0, ph, pltpu.roll(p, 1, 1))
        mp = jnp.where(lane == 0, mh, pltpu.roll(m, 1, 1))
        flux = (m + mp) * (p - pp)
        after = jnp.where(lane == BY - 1, (m + mh) * (ph - p), pltpu.roll(flux, BY - 1, 1))
        divergence = divergence + (after - flux)
        up[z] = c + (0.5 * step_length) * divergence
        return total + jnp.sum(m.reshape(16, 8, BY), axis=0)

    def p1_copies(h, start):
        for offset in Z_OFFSETS:
            peer = z_peer(offset)
            rows = pl.ds(pl.multiple_of(peer * 16 + h * 8, 8), 8)
            remote(
                up.at[pl.ds(start, CHUNK), rows, :],
                r1.at[h, pl.ds(gz * BZ + start, CHUNK)],
                p1_send,
                p1_recv.at[h],
                gz=peer,
            ).start()
        rows = pl.ds(pl.multiple_of(gz * 16 + h * 8, 8), 8)
        pltpu.make_async_copy(
            up.at[pl.ds(start, CHUNK), rows, :],
            r1.at[h, pl.ds(gz * BZ + start, CHUNK)],
            p1_recv.at[h],
        ).start()

    def stencil_chunk(k, total):
        start = k * CHUNK
        total = lax.fori_loop(start, start + CHUNK, stencil, total)
        p1_copies(0, start)
        return total

    total = lax.fori_loop(0, BZ // CHUNK, stencil_chunk, jnp.zeros((8, BY), F32))

    def second_half(k, carry):
        p1_copies(1, k * CHUNK)
        return carry

    lax.fori_loop(0, BZ // CHUNK, second_half, 0)

    ms[0] = total
    for s in (1, 2, 3):
        remote(ms.at[0], ms.at[s], m_send.at[0], m_recv.at[0], gx=(gx + s) % 4).start()

    def fill(k, carry):
        rows = pl.ds(pl.multiple_of(k * 32, 32), 32)
        waves[rows, :] = wave_of(iota((32, N), 0) + k * 32) + wave_of(iota((32, N), 1))
        return carry

    lax.fori_loop(0, N // 32, fill, 0)
    load_left.wait()
    load_right.wait()

    drain(ms.at[pl.ds(1, 3)], m_recv.at[0])
    mb[0] = ms[0] + ms[1] + ms[2] + ms[3]

    def spread(s, carry):
        a, b = plane_peer(s)
        remote(mb.at[0], mb.at[s], m_send.at[1], m_recv.at[1], gy=a, gz=b).start()
        return carry

    lax.fori_loop(1, 32, spread, 0)

    def fold(a, b):
        return thirds(a + b, 0), thirds(a - b, 0)

    def z_forward(h):
        source = r1.at[h].reshape(N * 8, BY)
        target = z1.at[h].reshape(N * 8, BY)

        def pair(k, carry):
            x0, x1 = 2 * k, 2 * k + 1

            def rows(base):
                return jnp.concatenate(
                    [
                        source[pl.ds(base * 8 + x0, HALF, stride=8), :],
                        source[pl.ds(base * 8 + x1, HALF, stride=8), :],
                    ],
                    axis=1,
                )

            plus, minus = fold(rows(0), rows(HALF))
            even = matmul(left[0], plus)
            odd = matmul(left[1], minus)
            for base, value in ((0, even), (HALF, odd)):
                target[pl.ds(base * 8 + x0, HALF, stride=8), :] = value[:, :BY]
                target[pl.ds(base * 8 + x1, HALF, stride=8), :] = value[:, BY:]
            return carry

        lax.fori_loop(0, 4, pair, 0)

    def gx_copies(source, target, send, recv, outward):
        for s in (1, 3, 2, 0):
            peer = (gx + s) % 4
            if outward:
                src, dst = source.at[pl.ds(peer * 128, 128)], target.at[gx]
            else:
                src, dst = source.at[peer], target.at[pl.ds(gx * 128, 128)]
            if s:
                remote(src, dst, send, recv, gx=peer).start()
            else:
                pltpu.make_async_copy(src, dst, recv).start()

    for h in (0, 1):
        drain(r1.at[h], p1_recv.at[h])
        z_forward(h)
        gx_copies(z1.at[h], a2.at[h], p2a_send, p2a_recv.at[h], True)

    def plane_part(h, p, a, b):
        rows = pl.ds(pl.multiple_of(b * 16 + h * 8, 8), 8)
        return pb.at[:, p, rows, pl.ds(pl.multiple_of(a * 128, 128), 128)]

    def p2b_copies(h, p):
        def send(s, carry):
            a, b = plane_peer(s)
            src = a2.at[h, :, (a * 8 + b) * 4 + p]
            remote(
                src, plane_part(h, p, gy, gz), p2b_send, p2b_recv.at[h * 4 + p], gy=a, gz=b
            ).start()
            return carry

        lax.fori_loop(1, 32, send, 0)
        pltpu.make_async_copy(
            a2.at[h, :, mine * 4 + p], plane_part(h, p, gy, gz), p2b_recv.at[h * 4 + p]
        ).start()

    def p3b_copies(h, p):
        def send(s, carry):
            a, b = plane_peer(s)
            remote(
                plane_part(h, p, a, b), a3.at[h, :, mine * 4 + p], p3b_send, p3b_recv.at[h], gy=a, gz=b
            ).start()
            return carry

        lax.fori_loop(1, 32, send, 0)
        pltpu.make_async_copy(
            plane_part(h, p, gy, gz), a3.at[h, :, mine * 4 + p], p3b_recv.at[h]
        ).start()

    for h in (0, 1):
        drain(a2.at[h], p2a_recv.at[h])

        def send_planes(p, carry):
            p2b_copies(h, p)
            return carry

        lax.fori_loop(0, 4, send_planes, 0)

    drain(mb.at[pl.ds(1, 31)], m_recv.at[1])
    mobility = jnp.sum(jnp.sum(mb[...], axis=0), keepdims=True)
    factor = (step_length * stiffness) * (mobility / float(N * N * N))

    def plane(p, carry):
        for h in (0, 1):
            drain(pb.at[:, p, pl.ds(0, 64), :], p2b_recv.at[h * 4 + p])
        wave_z = wave_of(gx * 128 + mine * 4 + p)

        def x_forward(k, carry):
            cols = pl.ds(pl.multiple_of(k * HALF, HALF), HALF)
            low = jnp.concatenate([pb[0, p, :, cols], pb[1, p, :, cols]], axis=0)
            high = jnp.concatenate([pb[2, p, :, cols], pb[3, p, :, cols]], axis=0)
            plus, minus = fold(low, high)
            work[pl.ds(0, HALF), cols] = matmul(left[0], plus)
            work[pl.ds(HALF, HALF), cols] = matmul(left[1], minus)
            return carry

        lax.fori_loop(0, 2, x_forward, 0)

        def y_both(k, carry):
            rows = pl.ds(pl.multiple_of(k * 128, 128), 128)
            a, b = work[rows, :HALF], work[rows, HALF:]
            parts = []
            for value, table, back, cols in (
                (a + b, 0, 0, pl.ds(0, HALF)),
                (a - b, 1, 2, pl.ds(HALF, HALF)),
            ):
                value = matmul(thirds(value, 1), right[table])
                wave = waves[rows, cols] + wave_z
                value = value / (1.0 + factor * (wave * wave))
                parts.append(matmul(thirds(value, 1), right[back]))
            work[rows, :HALF] = parts[0] + parts[1]
            work[rows, HALF:] = parts[0] - parts[1]
            return carry

        lax.fori_loop(0, 4, y_both, 0)

        def x_inverse(k, carry):
            cols = pl.ds(pl.multiple_of(k * HALF, HALF), HALF)
            a = matmul(left[0], thirds(work[pl.ds(0, HALF), cols], 0))
            b = matmul(left[2], thirds(work[pl.ds(HALF, HALF), cols], 0))
            plus, minus = a + b, a - b
            pb[0, p, :, cols], pb[1, p, :, cols] = plus[:128], plus[128:]
            pb[2, p, :, cols], pb[3, p, :, cols] = minus[:128], minus[128:]
            return carry

        lax.fori_loop(0, 2, x_inverse, 0)
        p3b_copies(0, p)
        return carry

    lax.fori_loop(0, 4, plane, 0)

    def rest(p, carry):
        p3b_copies(1, p)
        return carry

    lax.fori_loop(0, 4, rest, 0)

    for h in (0, 1):
        drain(a3.at[h], p3b_recv.at[h])
        gx_copies(a3.at[h], a4.at[h], p3a_send, p3a_recv.at[h], False)

    def z_inverse(h):
        source = a4.at[h].reshape(N * 8, BY)
        target = z4.at[h].reshape(N * 8, BY)

        def pair(k, carry):
            x0, x1 = 2 * k, 2 * k + 1

            def rows(base):
                return jnp.concatenate(
                    [
                        source[pl.ds(base * 8 + x0, HALF, stride=8), :],
                        source[pl.ds(base * 8 + x1, HALF, stride=8), :],
                    ],
                    axis=1,
                )

            a = matmul(left[0], thirds(rows(0), 0))
            b = matmul(left[2], thirds(rows(HALF), 0))
            for base, value in ((0, a + b), (HALF, a - b)):
                target[pl.ds(base * 8 + x0, HALF, stride=8), :] = value[:, :BY]
                target[pl.ds(base * 8 + x1, HALF, stride=8), :] = value[:, BY:]
            return carry

        lax.fori_loop(0, 4, pair, 0)

    for h in (0, 1):
        drain(a4.at[h], p3a_recv.at[h])
        z_inverse(h)
        rows = pl.ds(pl.multiple_of(gz * 16 + h * 8, 8), 8)

        def back(k, carry):
            start = k * CHUNK
            for offset in Z_OFFSETS:
                peer = z_peer(offset)
                remote(
                    z4.at[h, pl.ds(peer * BZ + start, CHUNK)],
                    o_ref.at[pl.ds(start, CHUNK), rows, :],
                    p4_send,
                    p4_recv.at[h],
                    gz=peer,
                ).start()
            pltpu.make_async_copy(
                z4.at[h, pl.ds(gz * BZ + start, CHUNK)],
                o_ref.at[pl.ds(start, CHUNK), rows, :],
                p4_recv.at[h],
            ).start()
            return carry

        lax.fori_loop(0, BZ // CHUNK, back, 0)

    for h in (0, 1):
        drain(o_ref.at[pl.ds(0, 32)], p4_recv.at[h])
    drain(up.at[pl.ds(0, 56)], p1_send)
    drain(ms.at[pl.ds(1, 3)], m_send.at[0])
    drain(mb.at[pl.ds(1, 31)], m_send.at[1])
    drain(z1.at[:, pl.ds(0, 384)], p2a_send)
    drain(up.at[pl.ds(0, 62)], p2b_send)
    drain(up.at[pl.ds(0, 62)], p3b_send)
    drain(z1.at[:, pl.ds(0, 384)], p3a_send)
    drain(up.at[pl.ds(0, 56)], p4_send)


def local(concentration):
    left, right = tables()
    vmem, dma = pltpu.VMEM, pltpu.SemaphoreType.DMA
    any_space = pl.BlockSpec(memory_space=pl.ANY)
    return pl.pallas_call(
        kernel,
        out_shape=jax.ShapeDtypeStruct((BZ, BX, BY), F32),
        in_specs=[any_space] * 3,
        out_specs=any_space,
        scratch_shapes=[
            vmem((BZ + 2, BX, BY), F32),
            vmem((2, BZ, BY), F32),
            vmem((2, BZ, BY), F32),
            vmem((BX, BY), F32),
            vmem((2, BX, BY), F32),
            vmem((BX, BY), F32),
            vmem((BZ, BX, BY), F32),
            vmem((2, N, 8, BY), F32),
            vmem((2, N, 8, BY), F32),
            vmem((2, 4, 128, 8, BY), F32),
            vmem((4, 4, BX, N), F32),
            vmem((2, 4, 128, 8, BY), F32),
            vmem((2, N, 8, BY), F32),
            vmem((2, N, 8, BY), F32),
            vmem((N, N), F32),
            vmem((N, N), F32),
            vmem((3, HALF, 3 * HALF), BF16),
            vmem((3, 3 * HALF, HALF), BF16),
            vmem((4, 8, BY), F32),
            vmem((32, 8, BY), F32),
            dma,
            dma((2,)),
            dma((6,)),
            dma((6,)),
            dma,
            dma((2,)),
            dma,
            dma((2,)),
            dma,
            dma((8,)),
            dma,
            dma((2,)),
            dma,
            dma((2,)),
            dma,
            dma((2,)),
            dma((2,)),
            dma((2,)),
        ],
        compiler_params=pltpu.CompilerParams(
            collective_id=0, has_side_effects=True, vmem_limit_bytes=60 * 2**20
        ),
    )(concentration, jnp.asarray(left), jnp.asarray(right))


def solution(mesh):
    spec = P("gz", "gx", "gy")
    return jax.shard_map(local, mesh=mesh, in_specs=(spec,), out_specs=spec, check_vma=False)
```

time: 502 us -> 227 us (0.45); the launches traced: 495 us -> 226 us
  Pallas kernels: 0 us -> 222 us
  blocking collectives: 181 us -> 0 us
  matrix products: 91 us -> 0 us
  other arithmetic: 73 us -> 0 us
  local copies, waits for them, and re-layouts: 76.6 us -> 4.7 us
  waiting for transfers between devices: 47.3 us -> 0 us
  starting transfers between devices: 24.8 us -> 0 us
    pallas_call x0 -> x1, Pallas kernels: none -> 222 us  [local(): pl.pallas_call(kernel, out_shape=jax.ShapeDtypeStruct((BZ, BX, BY), F32),...]
    all_to_all x2 -> x0, blocking collectives: 112 us -> none  [the longest x1 61.5 us: local(): lax.all_to_all(returning, GX_GY_GZ, split_axis=0, concat_axis=0, tiled=True)]
    dot_general x6 -> x0, matrix products: 91 us -> none  [the longest x2 33.7 us: plane_pass(): jnp.einsum('ij,rjy->riy', hartley_x, planes, precision=lax.Precision.HIGH...]
    psum x5 -> x0, blocking collectives: 69.3 us -> none  [by_axis(): return functools.reduce(lax.psum, axes, x)]
    all_to_all x2 -> x0, waiting for transfers between devices: 47.3 us -> none  [the longest x1 47.3 us: local(): pencil = lax.all_to_all(update, GZ, split_axis=1, concat_axis=0, tiled=True)]
    mul x6 -> x0, other arithmetic: 39.7 us -> none  [the longest x3 39.7 us: face_terms(): flux = 0.5 * (lower_mob + upper_mob) * (upper_pot - lower_pot)]
    unnamed x11 -> x1, local copies, waits for them, and re-layouts: 29 us -> 4.7 us
    dot_general x4 -> x0, local copies, waits for them, and re-layouts: 18.3 us -> none  [column_matmul(): jnp.dot(matrix, flat_columns, precision=lax.Precision.HIGHEST, preferred_...]
  transfers between devices with their start and end apart: 8 -> 0, of which waited for: 1 -> 0; matrix products, arithmetic and copies ran while one was open for 5% -> 0% of each run, Pallas kernels for 0% -> 0%
where the time goes in v1:
time: 227 us; the launch traced here: 226 us
  Pallas kernels  222 us (98%)
  local copies, waits for them, and re-layouts  4.7 us (2%)
    pallas_call x1, Pallas kernels, local(): pl.pallas_call(kernel, out_shape=jax.ShapeDtypeStruct((BZ, BX, BY), F32),...  222 us
    unnamed x1, local copies, waits for them, and re-layouts  4.7 us

profile of v1, /device:TPU:1, one launch (start us, length us, event | category | flops | bytes accessed | tf_op | source)
XLA Modules:
  0.0 226.4 jit_solution(605815602213519197)
XLA Ops:
  0.0 221.7 %shard_map.37 = f32[64,128,128]{2,1,0:T(8,128)} custom-call(f32[64,128,128]{2,1,0:T(8,128)} %c_ref.1, bf16[3,256,768]{2,1,0:T(8,128)(2,1)} %constant.4.clone.left_hbm, bf16[3,768,256]{2,1,0:T(8,128)(2,1)} %constant.5.clone.right_hbm), custom_call_target="tpu_custom_call" | custom-call | tf_op jit(solution)/shard_map/pallas_call | solution.py:482
  221.7 4.7 %copy.5 = f32[64,128,128]{2,1,0:T(8,128)} copy(f32[64,128,128]{2,1,0:T(8,128)} %shard_map.37) | data formatting | bytes 8388608

commit v2 on v1

v2 whole, which is shorter than its diff:
```python
import functools

import jax
import jax.numpy as jnp
import numpy as np
from jax import lax
from jax.experimental import pallas as pl
from jax.experimental.pallas import tpu as pltpu
from jax.sharding import PartitionSpec as P

MESH = pl.DeviceIdType.MESH
F32, BF16 = jnp.float32, jnp.bfloat16

step_length = 0.2
stiffness = 0.25

N = 512
HALF = N // 2
BZ, BX, BY = 64, 128, 128
CHUNKS = 4
X_OFFSETS = ((1, 0), (3, 0), (2, 0), (1, 1), (3, 1), (2, 1), (0, 1))


def split_table(matrix):
    high = matrix.astype(np.float32).astype(jnp.bfloat16)
    low = (matrix - high.astype(np.float64)).astype(np.float32).astype(jnp.bfloat16)
    return high, low


def tables():
    index = np.arange(N)
    angle = 2.0 * np.pi / N * (index[:, None] * index[None, :] % N)
    hartley = (np.cos(angle) + np.sin(angle)) / np.sqrt(N)
    even, odd = hartley[0::2, :HALF], hartley[1::2, :HALF]
    left, right = [], []
    for matrix in (even, odd, odd.T):
        high, low = split_table(matrix)
        left.append(np.concatenate([high, low, high], axis=1))
    for matrix in (even, odd.T, odd):
        high, low = split_table(matrix)
        right.append(np.concatenate([high, low, high], axis=0))
    return np.stack(left), np.stack(right)


def thirds(a, axis):
    high = a.astype(BF16)
    low = (a - high.astype(F32)).astype(BF16)
    return jnp.concatenate([high, high, low], axis=axis)


def matmul(a, b):
    return jnp.dot(a, b, preferred_element_type=F32)


def wave_of(position):
    true = jnp.where(position < HALF, 2 * position, 2 * position - (N - 1))
    folded = jnp.minimum(true, N - true).astype(F32)
    wave = (2.0 * np.pi / N) * folded
    return wave * wave


def iota(shape, dim):
    return lax.broadcasted_iota(jnp.int32, shape, dim)


def kernel(
    c_ref,
    left_hbm,
    right_hbm,
    o_ref,
    cz,
    xs,
    xr,
    ye,
    yr,
    yc,
    up,
    xa,
    ya,
    yb,
    xb,
    zb,
    ya2,
    xb2,
    xa2,
    yb2,
    waves,
    left,
    right,
    ms,
    mb,
    local_sem,
    table_sem,
    halo_send,
    halo_recv,
    sent,
    xa_sem,
    ya_sem,
    yb_sem,
    xb_sem,
    zb_sem,
    ya2_sem,
    xb2_sem,
    xa2_sem,
    yb2_sem,
    out_sem,
    m_send,
    m_recv,
):
    gx, gy, gz = lax.axis_index("gx"), lax.axis_index("gy"), lax.axis_index("gz")
    z_chip, x_low = gz // 2, gz % 2
    x_chip, core = (gy // 2) * 2 + x_low, gy % 2
    mine = gy * 2 + x_low

    def plane_peer(s):
        k = s % 16
        dx = k % 4
        dz = (k // 4 + dx) % 4
        px, pz, pc = (x_chip + dx) % 4, (z_chip + dz) % 4, (core + s // 16) % 2
        return (px // 2) * 2 + pc, pz * 2 + px % 2

    def row_peer(offset):
        px, pc = (x_chip + offset[0]) % 4, (core + offset[1]) % 2
        return (px // 2) * 2 + pc, px % 2

    def side_peer(s):
        dy = s % 4
        return (gx + dy) % 4, (z_chip + s // 4 + dy) % 4

    def remote(src, dst, send, recv, **where):
        return pltpu.make_async_remote_copy(
            src, dst, send, recv, device_id=where, device_id_type=MESH
        )

    def here(src, dst, recv):
        pltpu.make_async_copy(src, dst, recv).start()

    def drain(ref, sem):
        pltpu.make_async_copy(ref, ref, sem).wait()

    def lanes(block):
        return pl.ds(pl.multiple_of(block * 128, 128), 128)

    def rows(start, size):
        return pl.ds(pl.multiple_of(start, size), size)

    load = pltpu.make_async_copy(c_ref, cz.at[pl.ds(1, BZ)], local_sem)
    load.start()
    load_left = pltpu.make_async_copy(left_hbm, left, table_sem.at[0])
    load_right = pltpu.make_async_copy(right_hbm, right, table_sem.at[1])
    load_left.start()
    load_right.start()
    barrier = pltpu.get_barrier_semaphore()

    def greet(s, carry):
        a, b = plane_peer(s)
        pl.semaphore_signal(
            barrier, inc=1, device_id={"gy": a, "gz": b}, device_id_type=MESH
        )
        return carry

    def greet_side(s, carry):
        a, b = side_peer(s)
        pl.semaphore_signal(
            barrier, inc=1, device_id={"gx": a, "gz": b * 2 + x_low}, device_id_type=MESH
        )
        return carry

    lax.fori_loop(1, 32, greet, 0)
    lax.fori_loop(1, 16, greet_side, 0)
    load.wait()

    flat = cz.reshape((BZ + 2) * BX, BY)
    xs[0] = flat[pl.ds(BX, BZ, stride=BX), :]
    xs[1] = flat[pl.ds(BX + BX - 1, BZ, stride=BX), :]
    lane = iota((BX, BY), 1)

    def pack(z, acc):
        turned = pltpu.roll(cz[z + 1], 2 * z, 1)
        keep = (lane == 2 * z) | (lane == (2 * z + BY - 1) % BY)
        return jnp.where(keep, turned, acc)

    ye[...] = lax.fori_loop(0, BZ, pack, jnp.zeros((BX, BY), F32))

    pl.semaphore_wait(barrier, 46)
    halo = [
        remote(c_ref.at[pl.ds(BZ - 1, 1)], cz.at[pl.ds(0, 1)], halo_send.at[0], halo_recv.at[0], gz=(gz + 1) % 8),
        remote(c_ref.at[pl.ds(0, 1)], cz.at[pl.ds(BZ + 1, 1)], halo_send.at[1], halo_recv.at[1], gz=(gz + 7) % 8),
        remote(xs.at[1], xr.at[0], halo_send.at[2], halo_recv.at[2], gx=(gx + 1) % 4),
        remote(xs.at[0], xr.at[1], halo_send.at[3], halo_recv.at[3], gx=(gx + 3) % 4),
        remote(ye, yr.at[0], halo_send.at[4], halo_recv.at[4], gy=(gy + 1) % 4),
        remote(ye, yr.at[1], halo_send.at[5], halo_recv.at[5], gy=(gy + 3) % 4),
    ]
    for copy in halo:
        copy.start()
    for copy in halo:
        copy.wait()
    yc[...] = jnp.where(lane % 2 == 0, pltpu.roll(yr[0], 1, 1), pltpu.roll(yr[1], BY - 1, 1))

    row = iota((BX, BY), 0)

    def terms(c):
        square = c * c
        return square * c - c, 1.05 - square

    def stencil(z, total):
        c = cz[z + 1]
        p, m = terms(c)
        pz, mz = terms(cz[z + 2])
        divergence = (m + mz) * (pz - p)
        pz, mz = terms(cz[z])
        divergence = divergence - (m + mz) * (p - pz)
        ph, mh = terms(jnp.broadcast_to(xr[0, pl.ds(z, 1), :], (BX, BY)))
        pp = jnp.where(row == 0, ph, pltpu.roll(p, 1, 0))
        mp = jnp.where(row == 0, mh, pltpu.roll(m, 1, 0))
        flux = (m + mp) * (p - pp)
        ph, mh = terms(jnp.broadcast_to(xr[1, pl.ds(z, 1), :], (BX, BY)))
        after = jnp.where(row == BX - 1, (m + mh) * (ph - p), pltpu.roll(flux, BX - 1, 0))
        divergence = divergence + (after - flux)
        ph, mh = terms(pltpu.roll(yc[...], (BY - 2 * z) % BY, 1))
        pp = jnp.where(lane == 0, ph, pltpu.roll(p, 1, 1))
        mp = jnp.where(lane == 0, mh, pltpu.roll(m, 1, 1))
        flux = (m + mp) * (p - pp)
        after = jnp.where(lane == BY - 1, (m + mh) * (ph - p), pltpu.roll(flux, BY - 1, 1))
        divergence = divergence + (after - flux)
        up[z] = c + (0.5 * step_length) * divergence
        return total + jnp.sum(m.reshape(16, 8, BY), axis=0)

    def gx_copies(source, target, send, recv):
        for s in (1, 3, 2, 0):
            peer = (gx + s) % 4
            if s:
                remote(source(peer), target, sent.at[send], recv, gx=peer).start()
            else:
                here(source(gx), target, recv)

    def row_copies(source, target, send, recv):
        for offset in X_OFFSETS:
            a, low = row_peer(offset)
            remote(
                source(a, low), target, sent.at[send], recv, gy=a, gz=z_chip * 2 + low
            ).start()
        here(source(gy, x_low), target, recv)

    def first(k):
        gx_copies(
            lambda a: up.at[pl.ds(8 * k + 2 * a, 2)],
            xa.at[k, :, rows(gx * 128, 128), :],
            0,
            xa_sem.at[k],
        )
        row_copies(
            lambda a, low: up.at[32 + 8 * k + 2 * a + low],
            yb.at[k, x_low, :, lanes(gy)],
            1,
            yb_sem.at[k],
        )

    def second_a(k):
        row_copies(
            lambda a, low: xa.at[k, :, rows((2 * a + low) * 64, 64), :],
            ya.at[k, x_low, :, :, lanes(gy)],
            2,
            ya_sem.at[k],
        )

    def second_b(k):
        gx_copies(
            lambda a: yb.at[k, :, :, lanes(a)],
            xb.at[k, :, rows(gx * 128, 128), :],
            3,
            xb_sem.at[k],
        )

    def third_a(k):
        def part(h):
            def source(y, z):
                return ya.at[k, :, :, rows(16 * z + 8 * h, 8), lanes(y)]

            target = zb.at[h, pl.ds(2 * z_chip, 2), pl.ds(8 * k + 2 * gx, 2)]

            def send(s, carry):
                y, z = side_peer(s)
                remote(
                    source(y, z), target, sent.at[4], zb_sem.at[h], gx=y, gz=z * 2 + x_low
                ).start()
                return carry

            lax.fori_loop(1, 16, send, 0)
            here(source(gx, z_chip), target, zb_sem.at[h])

        part(0)
        part(1)

    def third_b(k):
        def part(h):
            def source(a, b):
                return xb.at[k, :, rows((2 * a + b % 2) * 64 + 16 * (b // 2) + 8 * h, 8), :]

            target = zb.at[h, pl.ds(2 * z_chip, 2), 32 + 8 * k + mine]

            def send(s, carry):
                a, b = plane_peer(s)
                remote(source(a, b), target, sent.at[5], zb_sem.at[h], gy=a, gz=b).start()
                return carry

            lax.fori_loop(1, 32, send, 0)
            here(source(gy, gz), target, zb_sem.at[h])

        part(0)
        part(1)

    def back_third(k, h):
        def source_a(y, z):
            return zb.at[h, pl.ds(2 * z, 2), pl.ds(8 * k + 2 * y, 2)]

        target_a = ya2.at[k, :, :, rows(16 * z_chip + 8 * h, 8), lanes(gx)]

        def send_a(s, carry):
            y, z = side_peer(s)
            remote(
                source_a(y, z), target_a, sent.at[6], ya2_sem.at[k], gx=y, gz=z * 2 + x_low
            ).start()
            return carry

        def source_b(a, b):
            return zb.at[h, pl.ds(2 * (b // 2), 2), 32 + 8 * k + 2 * a + b % 2]

        target_b = xb2.at[k, :, rows(mine * 64 + 16 * z_chip + 8 * h, 8), :]

        def send_b(s, carry):
            a, b = plane_peer(s)
            remote(source_b(a, b), target_b, sent.at[7], xb2_sem.at[k], gy=a, gz=b).start()
            return carry

        lax.fori_loop(1, 16, send_a, 0)
        here(source_a(gx, z_chip), target_a, ya2_sem.at[k])
        lax.fori_loop(1, 32, send_b, 0)
        here(source_b(gy, gz), target_b, xb2_sem.at[k])

    def back_second_a(k):
        row_copies(
            lambda a, low: ya2.at[k, low, :, :, lanes(a)],
            xa2.at[k, :, rows(mine * 64, 64), :],
            8,
            xa2_sem.at[k],
        )

    def back_second_b(k):
        gx_copies(
            lambda a: xb2.at[k, :, rows(a * 128, 128), :],
            yb2.at[k, :, :, lanes(gx)],
            9,
            yb2_sem.at[k],
        )

    def back_first_a(k):
        gx_copies(
            lambda a: xa2.at[k, :, rows(a * 128, 128), :],
            o_ref.at[pl.ds(8 * k + 2 * gx, 2)],
            10,
            out_sem,
        )

    def back_first_b(k):
        row_copies(
            lambda a, low: yb2.at[k, low, :, lanes(a)],
            o_ref.at[32 + 8 * k + mine],
            11,
            out_sem,
        )

    def x_pass(ref, inverse):
        low = jnp.concatenate([ref[0, :HALF], ref[1, :HALF]], axis=1)
        high = jnp.concatenate([ref[0, HALF:], ref[1, HALF:]], axis=1)
        if inverse:
            even = matmul(left[0], thirds(low, 0))
            odd = matmul(left[2], thirds(high, 0))
            low, high = even + odd, even - odd
        else:
            plus, minus = thirds(low + high, 0), thirds(low - high, 0)
            low, high = matmul(left[0], plus), matmul(left[1], minus)
        ref[0, :HALF], ref[1, :HALF] = low[:, :BY], low[:, BY:]
        ref[0, HALF:], ref[1, HALF:] = high[:, :BY], high[:, BY:]

    def y_pass(ref, inverse):
        flat = ref.reshape(256, N)

        def block(i, carry):
            part = rows(i * 128, 128)
            low, high = flat[part, :HALF], flat[part, HALF:]
            if inverse:
                even = matmul(thirds(low, 1), right[0])
                odd = matmul(thirds(high, 1), right[2])
                low, high = even + odd, even - odd
            else:
                plus, minus = thirds(low + high, 1), thirds(low - high, 1)
                low, high = matmul(plus, right[0]), matmul(minus, right[1])
            flat[part, :HALF] = low
            flat[part, HALF:] = high
            return carry

        lax.fori_loop(0, 2, block, 0)

    def stencil_chunk(k, total):
        total = lax.fori_loop(8 * k, 8 * k + 8, stencil, total)
        total = lax.fori_loop(32 + 8 * k, 40 + 8 * k, stencil, total)

        @pl.when(k < 2)
        def _():
            first(k)

        return total

    ms[0] = lax.fori_loop(0, CHUNKS, stencil_chunk, jnp.zeros((8, BY), F32))

    for s in (1, 2, 3):
        remote(ms.at[0], ms.at[s], m_send.at[0], m_recv.at[0], gx=(gx + s) % 4).start()

    def fill(k, carry):
        part = rows(k * 32, 32)
        waves[part, :] = wave_of(iota((32, BY), 0) + k * 32) + wave_of(iota((32, BY), 1) + gx * BY)
        return carry

    lax.fori_loop(0, N // 32, fill, 0)
    load_left.wait()
    load_right.wait()

    drain(ms.at[pl.ds(1, 3)], m_recv.at[0])
    mb[0] = ms[0] + ms[1] + ms[2] + ms[3]

    def spread(s, carry):
        a, b = plane_peer(s)
        remote(mb.at[0], mb.at[s], m_send.at[1], m_recv.at[1], gy=a, gz=b).start()
        return carry

    lax.fori_loop(1, 32, spread, 0)

    def forward(k, carry):
        @pl.when(k < CHUNKS)
        def _():
            drain(yb.at[k], yb_sem.at[k])
            y_pass(yb.at[k], False)
            second_b(k)
            drain(xa.at[k], xa_sem.at[k])
            x_pass(xa.at[k], False)
            second_a(k)

        @pl.when(k < CHUNKS - 2)
        def _():
            first(k + 2)

        @pl.when(k > 0)
        def _():
            drain(xb.at[k - 1], xb_sem.at[k - 1])
            x_pass(xb.at[k - 1], False)
            third_b(k - 1)
            drain(ya.at[k - 1], ya_sem.at[k - 1])
            y_pass(ya.at[k - 1], False)
            third_a(k - 1)

        return carry

    lax.fori_loop(0, CHUNKS + 1, forward, 0)

    drain(mb.at[pl.ds(1, 31)], m_recv.at[1])
    mobility = jnp.sum(jnp.sum(mb[...], axis=0), keepdims=True)
    factor = (step_length * stiffness) * (mobility / float(N * N * N))

    def z_stage(h):
        drain(zb.at[h], zb_sem.at[h])
        field = zb.at[h].reshape(N * 8, BY)

        def pair(i, carry):
            x0, x1 = 2 * i, 2 * i + 1

            def take(base):
                return jnp.concatenate(
                    [
                        field[pl.ds(base * 8 + x0, HALF, stride=8), :],
                        field[pl.ds(base * 8 + x1, HALF, stride=8), :],
                    ],
                    axis=1,
                )

            position = mine * 64 + 16 * z_chip + 8 * h
            wave0, wave1 = wave_of(position + x0), wave_of(position + x1)
            low, high = take(0), take(HALF)
            parts = []
            for value, table, back, base in (
                (low + high, 0, 0, 0),
                (low - high, 1, 2, HALF),
            ):
                value = matmul(left[table], thirds(value, 0))
                wave = waves[pl.ds(base, HALF), :]
                wave = jnp.concatenate([wave + wave0, wave + wave1], axis=1)
                value = value / (1.0 + factor * (wave * wave))
                parts.append(matmul(left[back], thirds(value, 0)))
            for base, value in ((0, parts[0] + parts[1]), (HALF, parts[0] - parts[1])):
                field[pl.ds(base * 8 + x0, HALF, stride=8), :] = value[:, :BY]
                field[pl.ds(base * 8 + x1, HALF, stride=8), :] = value[:, BY:]
            return carry

        lax.fori_loop(0, 4, pair, 0)
        back_third(0, h)

    z_stage(0)
    z_stage(1)
    back_third(1, 0)
    back_third(1, 1)

    def inverse(k, carry):
        @pl.when(k < CHUNKS)
        def _():
            drain(ya2.at[k], ya2_sem.at[k])
            y_pass(ya2.at[k], True)
            back_second_a(k)
            drain(xb2.at[k], xb2_sem.at[k])
            x_pass(xb2.at[k], True)
            back_second_b(k)

        @pl.when(k < CHUNKS - 2)
        def _():
            back_third(k + 2, 0)
            back_third(k + 2, 1)

        @pl.when(k > 0)
        def _():
            drain(xa2.at[k - 1], xa2_sem.at[k - 1])
            x_pass(xa2.at[k - 1], True)
            back_first_a(k - 1)
            drain(yb2.at[k - 1], yb2_sem.at[k - 1])
            y_pass(yb2.at[k - 1], True)
            back_first_b(k - 1)

        return carry

    lax.fori_loop(0, CHUNKS + 1, inverse, 0)
    drain(o_ref, out_sem)

    for i, layers in enumerate((24, 28, 28, 24, 30, 31, 30, 31, 28, 24, 24, 28)):
        drain(up.at[pl.ds(0, layers)], sent.at[i])
    drain(ms.at[pl.ds(1, 3)], m_send.at[0])
    drain(mb.at[pl.ds(1, 31)], m_send.at[1])


def local(concentration):
    left, right = tables()
    vmem, dma = pltpu.VMEM, pltpu.SemaphoreType.DMA
    any_space = pl.BlockSpec(memory_space=pl.ANY)
    x_field = vmem((CHUNKS, 2, N, BY), F32)
    ya_field = vmem((CHUNKS, 2, 2, 64, N), F32)
    yb_field = vmem((CHUNKS, 2, BX, N), F32)
    return pl.pallas_call(
        kernel,
        out_shape=jax.ShapeDtypeStruct((BZ, BX, BY), F32),
        in_specs=[any_space] * 3,
        out_specs=any_space,
        scratch_shapes=[
            vmem((BZ + 2, BX, BY), F32),
            vmem((2, BZ, BY), F32),
            vmem((2, BZ, BY), F32),
            vmem((BX, BY), F32),
            vmem((2, BX, BY), F32),
            vmem((BX, BY), F32),
            vmem((BZ, BX, BY), F32),
            x_field,
            ya_field,
            yb_field,
            x_field,
            vmem((2, 8, BZ, 8, BY), F32),
            ya_field,
            x_field,
            x_field,
            yb_field,
            vmem((N, BY), F32),
            vmem((3, HALF, 3 * HALF), BF16),
            vmem((3, 3 * HALF, HALF), BF16),
            vmem((4, 8, BY), F32),
            vmem((32, 8, BY), F32),
            dma,
            dma((2,)),
            dma((6,)),
            dma((6,)),
            dma((12,)),
            dma((CHUNKS,)),
            dma((CHUNKS,)),
            dma((CHUNKS,)),
            dma((CHUNKS,)),
            dma((2,)),
            dma((CHUNKS,)),
            dma((CHUNKS,)),
            dma((CHUNKS,)),
            dma((CHUNKS,)),
            dma,
            dma((2,)),
            dma((2,)),
        ],
        compiler_params=pltpu.CompilerParams(
            collective_id=0, has_side_effects=True, vmem_limit_bytes=60 * 2**20
        ),
    )(concentration, jnp.asarray(left), jnp.asarray(right))


def solution(mesh):
    spec = P("gz", "gx", "gy")
    return jax.shard_map(local, mesh=mesh, in_specs=(spec,), out_specs=spec, check_vma=False)
```

time: 227 us -> 197 us (0.87)
  Pallas kernels: 222 us -> 192 us
    pallas_call x1, Pallas kernels: 222 us -> 192 us  [local(): pl.pallas_call(kernel, out_shape=jax.ShapeDtypeStruct((BZ, BX, BY), F32),...]
where the time goes in v2:
time: 197 us
  Pallas kernels  192 us (97%)
  local copies, waits for them, and re-layouts  4.7 us (2%)
    pallas_call x1, Pallas kernels, local(): pl.pallas_call(kernel, out_shape=jax.ShapeDtypeStruct((BZ, BX, BY), F32),...  192 us
    unnamed x1, local copies, waits for them, and re-layouts  4.7 us

profile of v2, /device:TPU:1, one launch (start us, length us, event | category | flops | bytes accessed | tf_op | source)
XLA Modules:
  0.0 196.6 jit_solution(13640189347898657066)
XLA Ops:
  0.0 191.9 %shard_map.37 = f32[64,128,128]{2,1,0:T(8,128)} custom-call(f32[64,128,128]{2,1,0:T(8,128)} %c_ref.1, bf16[3,256,768]{2,1,0:T(8,128)(2,1)} %constant.4.clone.left_hbm, bf16[3,768,256]{2,1,0:T(8,128)(2,1)} %constant.5.clone.right_hbm), custom_call_target="tpu_custom_call" | custom-call | tf_op jit(solution)/shard_map/pallas_call | solution.py:554
  191.9 4.7 %copy.5 = f32[64,128,128]{2,1,0:T(8,128)} copy(f32[64,128,128]{2,1,0:T(8,128)} %shard_map.37) | data formatting | bytes 8388608

commit v3 on v2

--- a/solution.py
+++ b/solution.py
@@ -18,6 +18,14 @@
 HALF = N // 2
 BZ, BX, BY = 64, 128, 128
 CHUNKS = 4
+FORWARD = (
+    ("F", 0), ("F", 1), ("I", 2), ("I", 3), ("G", 0), ("P", 0), ("S", 0), ("F", 2), ("S", 1),
+    ("M", 0), ("H", 0), ("F", 3), ("T", 0), ("S", 2), ("T", 1), ("S", 3), ("T", 2), ("T", 3),
+)
+BACKWARD = (
+    ("Z", 0), ("Z", 1), ("T", 1), ("S", 0), ("T", 2), ("S", 1), ("T", 3), ("F", 0), ("S", 2),
+    ("F", 1), ("S", 3), ("F", 2), ("F", 3),
+)
 X_OFFSETS = ((1, 0), (3, 0), (2, 0), (1, 1), (3, 1), (2, 1), (0, 1))
 
 
@@ -35,10 +43,10 @@
     left, right = [], []
     for matrix in (even, odd, odd.T):
         high, low = split_table(matrix)
-        left.append(np.concatenate([high, low, high], axis=1))
+        left.append(np.concatenate([high, low], axis=1))
     for matrix in (even, odd.T, odd):
         high, low = split_table(matrix)
-        right.append(np.concatenate([high, low, high], axis=0))
+        right.append(np.concatenate([high, low], axis=0))
     return np.stack(left), np.stack(right)
 
 
@@ -74,6 +82,7 @@
     ye,
     yr,
     yc,
+    zr,
     up,
     xa,
     ya,
@@ -106,6 +115,7 @@
     out_sem,
     m_send,
     m_recv,
+    ready,
 ):
     gx, gy, gz = lax.axis_index("gx"), lax.axis_index("gy"), lax.axis_index("gz")
     z_chip, x_low = gz // 2, gz % 2
@@ -144,87 +154,116 @@
     def rows(start, size):
         return pl.ds(pl.multiple_of(start, size), size)
 
-    load = pltpu.make_async_copy(c_ref, cz.at[pl.ds(1, BZ)], local_sem)
+    load = pltpu.make_async_copy(c_ref, cz, local_sem)
     load.start()
-    load_left = pltpu.make_async_copy(left_hbm, left, table_sem.at[0])
-    load_right = pltpu.make_async_copy(right_hbm, right, table_sem.at[1])
-    load_left.start()
-    load_right.start()
+    pair, third = pl.ds(0, N), pl.ds(N, HALF)
+    loads = [
+        pltpu.make_async_copy(left_hbm, left.at[:, :, pair], table_sem.at[0]),
+        pltpu.make_async_copy(left_hbm.at[:, :, pl.ds(0, HALF)], left.at[:, :, third], table_sem.at[1]),
+        pltpu.make_async_copy(right_hbm, right.at[:, pair], table_sem.at[2]),
+        pltpu.make_async_copy(right_hbm.at[:, pl.ds(0, HALF)], right.at[:, third], table_sem.at[3]),
+    ]
+    for copy in loads:
+        copy.start()
     barrier = pltpu.get_barrier_semaphore()
 
-    def greet(s, carry):
-        a, b = plane_peer(s)
+    for offset in X_OFFSETS:
+        a, low = row_peer(offset)
         pl.semaphore_signal(
-            barrier, inc=1, device_id={"gy": a, "gz": b}, device_id_type=MESH
-        )
-        return carry
-
-    def greet_side(s, carry):
-        a, b = side_peer(s)
+            barrier, inc=1, device_id={"gy": a, "gz": z_chip * 2 + low}, device_id_type=MESH
+        )
+    across = ((z_chip + 3 - 2 * x_low) % 4) * 2 + 1 - x_low
+    columns = [((z_chip + s) % 4) * 2 + x_low for s in (1, 2, 3)]
+    for s in (1, 2, 3):
         pl.semaphore_signal(
-            barrier, inc=1, device_id={"gx": a, "gz": b * 2 + x_low}, device_id_type=MESH
-        )
-        return carry
-
-    lax.fori_loop(1, 32, greet, 0)
-    lax.fori_loop(1, 16, greet_side, 0)
+            barrier, inc=1, device_id={"gx": (gx + s) % 4}, device_id_type=MESH
+        )
+    for other in columns + [across]:
+        pl.semaphore_signal(barrier, inc=1, device_id={"gz": other}, device_id_type=MESH)
     load.wait()
 
-    flat = cz.reshape((BZ + 2) * BX, BY)
-    xs[0] = flat[pl.ds(BX, BZ, stride=BX), :]
-    xs[1] = flat[pl.ds(BX + BX - 1, BZ, stride=BX), :]
+    flat = cz.reshape(BZ * BX, BY)
+    xs[0] = flat[pl.ds(0, BZ, stride=BX), :]
+    xs[1] = flat[pl.ds(BX - 1, BZ, stride=BX), :]
     lane = iota((BX, BY), 1)
+    row = iota((BX, BY), 0)
 
     def pack(z, acc):
-        turned = pltpu.roll(cz[z + 1], 2 * z, 1)
+        turned = pltpu.roll(cz[z], 2 * z, 1)
         keep = (lane == 2 * z) | (lane == (2 * z + BY - 1) % BY)
         return jnp.where(keep, turned, acc)
 
-    ye[...] = lax.fori_loop(0, BZ, pack, jnp.zeros((BX, BY), F32))
-
-    pl.semaphore_wait(barrier, 46)
+    ye[...] = lax.fori_loop(0, BZ, pack, jnp.zeros((BX, BY), F32), unroll=4)
+
+    def terms(c):
+        square = c * c
+        return square * c - c, 1.05 - square
+
+    def inner(z, total):
+        c = cz[z]
+        p, m = terms(c)
+        pz, mz = terms(cz[jnp.minimum(z + 1, BZ - 1)])
+        divergence = (m + mz) * (pz - p)
+        pz, mz = terms(cz[jnp.maximum(z - 1, 0)])
+        divergence = divergence - (m + mz) * (p - pz)
+        before = jnp.where(row == 0, p, pltpu.roll(p, 1, 0))
+        flux = (m + pltpu.roll(m, 1, 0)) * (p - before)
+        divergence = divergence + (pltpu.roll(flux, BX - 1, 0) - flux)
+        before = jnp.where(lane == 0, p, pltpu.roll(p, 1, 1))
+        flux = (m + pltpu.roll(m, 1, 1)) * (p - before)
+        divergence = divergence + (pltpu.roll(flux, BY - 1, 1) - flux)
+        up[z] = c + (0.5 * step_length) * divergence
+        return total + jnp.sum(m.reshape(16, 8, BY), axis=0)
+
+    def inner_chunk(k):
+        total = lax.fori_loop(8 * k, 8 * k + 8, inner, jnp.zeros((8, BY), F32), unroll=2)
+        total = lax.fori_loop(32 + 8 * k, 40 + 8 * k, inner, total, unroll=2)
+        ms[0] = total if k == 0 else ms[0] + total
+
+    pl.semaphore_wait(barrier, 14)
     halo = [
-        remote(c_ref.at[pl.ds(BZ - 1, 1)], cz.at[pl.ds(0, 1)], halo_send.at[0], halo_recv.at[0], gz=(gz + 1) % 8),
-        remote(c_ref.at[pl.ds(0, 1)], cz.at[pl.ds(BZ + 1, 1)], halo_send.at[1], halo_recv.at[1], gz=(gz + 7) % 8),
+        remote(ye, yr.at[0], halo_send.at[4], halo_recv.at[4], gy=(gy + 1) % 4),
+        remote(ye, yr.at[1], halo_send.at[5], halo_recv.at[5], gy=(gy + 3) % 4),
+        remote(c_ref.at[BZ - 1], zr.at[0], halo_send.at[0], halo_recv.at[0], gz=(gz + 1) % 8),
+        remote(c_ref.at[0], zr.at[1], halo_send.at[1], halo_recv.at[1], gz=(gz + 7) % 8),
         remote(xs.at[1], xr.at[0], halo_send.at[2], halo_recv.at[2], gx=(gx + 1) % 4),
         remote(xs.at[0], xr.at[1], halo_send.at[3], halo_recv.at[3], gx=(gx + 3) % 4),
-        remote(ye, yr.at[0], halo_send.at[4], halo_recv.at[4], gy=(gy + 1) % 4),
-        remote(ye, yr.at[1], halo_send.at[5], halo_recv.at[5], gy=(gy + 3) % 4),
     ]
     for copy in halo:
         copy.start()
+    inner_chunk(0)
+    inner_chunk(1)
     for copy in halo:
         copy.wait()
-    yc[...] = jnp.where(lane % 2 == 0, pltpu.roll(yr[0], 1, 1), pltpu.roll(yr[1], BY - 1, 1))
-
-    row = iota((BX, BY), 0)
-
-    def terms(c):
-        square = c * c
-        return square * c - c, 1.05 - square
-
-    def stencil(z, total):
-        c = cz[z + 1]
-        p, m = terms(c)
-        pz, mz = terms(cz[z + 2])
-        divergence = (m + mz) * (pz - p)
-        pz, mz = terms(cz[z])
-        divergence = divergence - (m + mz) * (p - pz)
-        ph, mh = terms(jnp.broadcast_to(xr[0, pl.ds(z, 1), :], (BX, BY)))
-        pp = jnp.where(row == 0, ph, pltpu.roll(p, 1, 0))
-        mp = jnp.where(row == 0, mh, pltpu.roll(m, 1, 0))
-        flux = (m + mp) * (p - pp)
-        ph, mh = terms(jnp.broadcast_to(xr[1, pl.ds(z, 1), :], (BX, BY)))
-        after = jnp.where(row == BX - 1, (m + mh) * (ph - p), pltpu.roll(flux, BX - 1, 0))
-        divergence = divergence + (after - flux)
-        ph, mh = terms(pltpu.roll(yc[...], (BY - 2 * z) % BY, 1))
-        pp = jnp.where(lane == 0, ph, pltpu.roll(p, 1, 1))
-        mp = jnp.where(lane == 0, mh, pltpu.roll(m, 1, 1))
-        flux = (m + mp) * (p - pp)
-        after = jnp.where(lane == BY - 1, (m + mh) * (ph - p), pltpu.roll(flux, BY - 1, 1))
-        divergence = divergence + (after - flux)
-        up[z] = c + (0.5 * step_length) * divergence
-        return total + jnp.sum(m.reshape(16, 8, BY), axis=0)
+
+    def inflow(inside, outside):
+        p, m = terms(inside)
+        ph, mh = terms(outside)
+        return (0.5 * step_length) * ((m + mh) * (ph - p))
+
+    yc[...] = inflow(
+        ye[...], jnp.where(lane % 2 == 0, pltpu.roll(yr[0], 1, 1), pltpu.roll(yr[1], BY - 1, 1))
+    )
+    xr[0] = inflow(xs[0], xr[0])
+    xr[1] = inflow(xs[1], xr[1])
+    edge = (lane == 0) | (lane == BY - 1)
+    layers = up.reshape(BZ * BX, BY)
+
+    def outer(z, carry):
+        turned = pltpu.roll(yc[...], (BY - 2 * z) % BY, 1)
+        up[z] = up[z] + jnp.where(edge, turned, 0.0)
+        return carry
+
+    def outer_chunk(k):
+        if k == 0:
+            up[0] = up[0] + inflow(cz[0], zr[0])
+        if k == CHUNKS - 1:
+            up[BZ - 1] = up[BZ - 1] + inflow(cz[BZ - 1], zr[1])
+        for base in (8 * k, 32 + 8 * k):
+            for side, place in ((0, 0), (1, BX - 1)):
+                part = pl.ds(base * BX + place, 8, stride=BX)
+                layers[part, :] = layers[part, :] + xr[side, pl.ds(base, 8), :]
+            lax.fori_loop(base, base + 8, outer, 0, unroll=4)
 
     def gx_copies(source, target, send, recv):
         for s in (1, 3, 2, 0):
@@ -272,7 +311,7 @@
             xb_sem.at[k],
         )
 
-    def third_a(k):
+    def third_a(k, h_):
         def part(h):
             def source(y, z):
                 return ya.at[k, :, :, rows(16 * z + 8 * h, 8), lanes(y)]
@@ -289,10 +328,9 @@
             lax.fori_loop(1, 16, send, 0)
             here(source(gx, z_chip), target, zb_sem.at[h])
 
-        part(0)
-        part(1)
-
-    def third_b(k):
+        part(h_)
+
+    def third_b(k, h_):
         def part(h):
             def source(a, b):
                 return xb.at[k, :, rows((2 * a + b % 2) * 64 + 16 * (b // 2) + 8 * h, 8), :]
@@ -307,8 +345,7 @@
             lax.fori_loop(1, 32, send, 0)
             here(source(gy, gz), target, zb_sem.at[h])
 
-        part(0)
-        part(1)
+        part(h_)
 
     def back_third(k, h):
         def source_a(y, z):
@@ -402,66 +439,60 @@
 
         lax.fori_loop(0, 2, block, 0)
 
-    def stencil_chunk(k, total):
-        total = lax.fori_loop(8 * k, 8 * k + 8, stencil, total)
-        total = lax.fori_loop(32 + 8 * k, 40 + 8 * k, stencil, total)
-
-        @pl.when(k < 2)
-        def _():
-            first(k)
-
-        return total
-
-    ms[0] = lax.fori_loop(0, CHUNKS, stencil_chunk, jnp.zeros((8, BY), F32))
-
-    for s in (1, 2, 3):
-        remote(ms.at[0], ms.at[s], m_send.at[0], m_recv.at[0], gx=(gx + s) % 4).start()
+    def start(k):
+        outer_chunk(k)
+        first(k)
+
+    def second(k):
+        drain(yb.at[k], yb_sem.at[k])
+        y_pass(yb.at[k], False)
+        second_b(k)
+        drain(xa.at[k], xa_sem.at[k])
+        x_pass(xa.at[k], False)
+        second_a(k)
+
+    def meet(k):
+        for other in columns:
+            pl.semaphore_signal(ready, inc=1, device_id={"gz": other}, device_id_type=MESH)
+        pl.semaphore_wait(ready, 3)
+
+    def third(k):
+        drain(xb.at[k], xb_sem.at[k])
+        x_pass(xb.at[k], False)
+        third_b(k, 0)
+        drain(ya.at[k], ya_sem.at[k])
+        y_pass(ya.at[k], False)
+        third_a(k, 0)
+        third_b(k, 1)
+        third_a(k, 1)
+
+    def gather(k):
+        for s in (1, 2, 3):
+            remote(ms.at[0], ms.at[s], m_send.at[0], m_recv.at[0], gx=(gx + s) % 4).start()
+
+    def spread(s, carry):
+        a, b = plane_peer(s)
+        remote(mb.at[0], mb.at[s], m_send.at[1], m_recv.at[1], gy=a, gz=b).start()
+        return carry
+
+    def share(k):
+        drain(ms.at[pl.ds(1, 3)], m_recv.at[0])
+        mb[0] = ms[0] + ms[1] + ms[2] + ms[3]
+        lax.fori_loop(1, 32, spread, 0)
 
     def fill(k, carry):
         part = rows(k * 32, 32)
         waves[part, :] = wave_of(iota((32, BY), 0) + k * 32) + wave_of(iota((32, BY), 1) + gx * BY)
         return carry
 
-    lax.fori_loop(0, N // 32, fill, 0)
-    load_left.wait()
-    load_right.wait()
-
-    drain(ms.at[pl.ds(1, 3)], m_recv.at[0])
-    mb[0] = ms[0] + ms[1] + ms[2] + ms[3]
-
-    def spread(s, carry):
-        a, b = plane_peer(s)
-        remote(mb.at[0], mb.at[s], m_send.at[1], m_recv.at[1], gy=a, gz=b).start()
-        return carry
-
-    lax.fori_loop(1, 32, spread, 0)
-
-    def forward(k, carry):
-        @pl.when(k < CHUNKS)
-        def _():
-            drain(yb.at[k], yb_sem.at[k])
-            y_pass(yb.at[k], False)
-            second_b(k)
-            drain(xa.at[k], xa_sem.at[k])
-            x_pass(xa.at[k], False)
-            second_a(k)
-
-        @pl.when(k < CHUNKS - 2)
-        def _():
-            first(k + 2)
-
-        @pl.when(k > 0)
-        def _():
-            drain(xb.at[k - 1], xb_sem.at[k - 1])
-            x_pass(xb.at[k - 1], False)
-            third_b(k - 1)
-            drain(ya.at[k - 1], ya_sem.at[k - 1])
-            y_pass(ya.at[k - 1], False)
-            third_a(k - 1)
-
-        return carry
-
-    lax.fori_loop(0, CHUNKS + 1, forward, 0)
+    def prepare(k):
+        lax.fori_loop(0, N // 32, fill, 0)
+        for copy in loads:
+            copy.wait()
+
+    steps = dict(F=start, I=inner_chunk, S=second, T=third, M=meet, G=gather, H=share, P=prepare)
+    for name, k in FORWARD:
+        steps[name](k)
 
     drain(mb.at[pl.ds(1, 31)], m_recv.at[1])
     mobility = jnp.sum(jnp.sum(mb[...], axis=0), keepdims=True)
@@ -504,42 +535,33 @@
         lax.fori_loop(0, 4, pair, 0)
         back_third(0, h)
 
-    z_stage(0)
-    z_stage(1)
-    back_third(1, 0)
-    back_third(1, 1)
-
-    def inverse(k, carry):
-        @pl.when(k < CHUNKS)
-        def _():
-            drain(ya2.at[k], ya2_sem.at[k])
-            y_pass(ya2.at[k], True)
-            back_second_a(k)
-            drain(xb2.at[k], xb2_sem.at[k])
-            x_pass(xb2.at[k], True)
-            back_second_b(k)
-
-        @pl.when(k < CHUNKS - 2)
-        def _():
-            back_third(k + 2, 0)
-            back_third(k + 2, 1)
-
-        @pl.when(k > 0)
-        def _():
-            drain(xa2.at[k - 1], xa2_sem.at[k - 1])
-            x_pass(xa2.at[k - 1], True)
-            back_first_a(k - 1)
-            drain(yb2.at[k - 1], yb2_sem.at[k - 1])
-            y_pass(yb2.at[k - 1], True)
-            back_first_b(k - 1)
-
-        return carry
-
-    lax.fori_loop(0, CHUNKS + 1, inverse, 0)
+    def back_both(k):
+        back_third(k, 0)
+        back_third(k, 1)
+
+    def inverse_two(k):
+        drain(ya2.at[k], ya2_sem.at[k])
+        y_pass(ya2.at[k], True)
+        back_second_a(k)
+        drain(xb2.at[k], xb2_sem.at[k])
+        x_pass(xb2.at[k], True)
+        back_second_b(k)
+
+    def inverse_one(k):
+        drain(xa2.at[k], xa2_sem.at[k])
+        x_pass(xa2.at[k], True)
+        back_first_a(k)
+        drain(yb2.at[k], yb2_sem.at[k])
+        y_pass(yb2.at[k], True)
+        back_first_b(k)
+
+    steps = dict(Z=z_stage, T=back_both, S=inverse_two, F=inverse_one)
+    for name, k in BACKWARD:
+        steps[name](k)
     drain(o_ref, out_sem)
 
-    for i, layers in enumerate((24, 28, 28, 24, 30, 31, 30, 31, 28, 24, 24, 28)):
-        drain(up.at[pl.ds(0, layers)], sent.at[i])
+    for i, count in enumerate((24, 28, 28, 24, 30, 31, 30, 31, 28, 24, 24, 28)):
+        drain(up.at[pl.ds(0, count)], sent.at[i])
     drain(ms.at[pl.ds(1, 3)], m_send.at[0])
     drain(mb.at[pl.ds(1, 31)], m_send.at[1])
 
@@ -548,21 +570,23 @@
     left, right = tables()
     vmem, dma = pltpu.VMEM, pltpu.SemaphoreType.DMA
     any_space = pl.BlockSpec(memory_space=pl.ANY)
+    hbm = pl.BlockSpec(memory_space=pltpu.HBM)
     x_field = vmem((CHUNKS, 2, N, BY), F32)
     ya_field = vmem((CHUNKS, 2, 2, 64, N), F32)
     yb_field = vmem((CHUNKS, 2, BX, N), F32)
     return pl.pallas_call(
         kernel,
         out_shape=jax.ShapeDtypeStruct((BZ, BX, BY), F32),
-        in_specs=[any_space] * 3,
+        in_specs=[hbm] * 3,
         out_specs=any_space,
         scratch_shapes=[
-            vmem((BZ + 2, BX, BY), F32),
+            vmem((BZ, BX, BY), F32),
             vmem((2, BZ, BY), F32),
             vmem((2, BZ, BY), F32),
             vmem((BX, BY), F32),
             vmem((2, BX, BY), F32),
             vmem((BX, BY), F32),
+            vmem((2, BX, BY), F32),
             vmem((BZ, BX, BY), F32),
             x_field,
             ya_field,
@@ -579,7 +603,7 @@
             vmem((4, 8, BY), F32),
             vmem((32, 8, BY), F32),
             dma,
-            dma((2,)),
+            dma((4,)),
             dma((6,)),
             dma((6,)),
             dma((12,)),
@@ -595,9 +619,10 @@
             dma,
             dma((2,)),
             dma((2,)),
+            pltpu.SemaphoreType.REGULAR,
         ],
         compiler_params=pltpu.CompilerParams(
-            collective_id=0, has_side_effects=True, vmem_limit_bytes=60 * 2**20
+            collective_id=0, has_side_effects=True, vmem_limit_bytes=44 * 2**20
         ),
     )(concentration, jnp.asarray(left), jnp.asarray(right))
 

time: 197 us -> 185 us (0.939)
  Pallas kernels: 192 us -> 179 us
    pallas_call x1, Pallas kernels: 192 us -> 179 us  [local(): pl.pallas_call(kernel, out_shape=jax.ShapeDtypeStruct((BZ, BX, BY), F32),...]
    unnamed x1 -> x7, local copies, waits for them, and re-layouts: 4.7 us -> 6.47 us
where the time goes in v3:
time: 185 us
  Pallas kernels  179 us (97%)
  local copies, waits for them, and re-layouts  6.47 us (3%)
    pallas_call x1, Pallas kernels, local(): pl.pallas_call(kernel, out_shape=jax.ShapeDtypeStruct((BZ, BX, BY), F32),...  179 us
    unnamed x7, local copies, waits for them, and re-layouts  6.47 us

profile of v3, /device:TPU:1, one launch (start us, length us, event | category | flops | bytes accessed | tf_op | source)
XLA Modules:
  0.0 185.2 jit_solution(7749882932447993473)
XLA Ops:
  0.0 0.0 copy-start
  0.0 2.2 %copy-done = f32[64,128,128]{2,1,0:T(8,128)S(1)} copy-done((f32[64,128,128]{2,1,0:T(8,128)S(1)}, f32[64,128,128]{2,1,0:T(8,128)}, u32[]{:S(2)}) %copy-start) | copy-done | bytes 4194328
  2.2 0.0 copy-start.1
  2.2 1.1 copy-done.1
  3.3 0.0 copy-start.2
  3.3 1.1 copy-done.2
  4.5 178.7 %shard_map.37 = f32[64,128,128]{2,1,0:T(8,128)S(1)} custom-call(f32[64,128,128]{2,1,0:T(8,128)S(1)} %copy-done, bf16[3,256,512]{2,1,0:T(8,128)(2,1)S(1)} %copy-done.2, bf16[3,512,256]{2,1,0:T(8,128)(2,1)S(1)} %copy-done.1), custom_call_target="tpu_custom_call" | custom-call | tf_op jit(solution)/shard_map/pallas_call | solution.py:577
  183.2 2.0 %copy.5 = f32[64,128,128]{2,1,0:T(8,128)} copy(f32[64,128,128]{2,1,0:T(8,128)S(1)} %shard_map.37) | data formatting | bytes 8388608
Async XLA Ops:
  0.0 2.2 %copy-start = (f32[64,128,128]{2,1,0:T(8,128)S(1)}, f32[64,128,128]{2,1,0:T(8,128)}, u32[]{:S(2)}) copy-start(f32[64,128,128]{2,1,0:T(8,128)} %c_ref.1) | copy-start | bytes 12582916
  2.2 1.1 copy-start.1
  3.3 1.1 copy-start.2

commit v4 on v3

--- a/solution.py
+++ b/solution.py
@@ -23,7 +23,7 @@
     ("M", 0), ("H", 0), ("F", 3), ("T", 0), ("S", 2), ("T", 1), ("S", 3), ("T", 2), ("T", 3),
 )
 BACKWARD = (
-    ("Z", 0), ("Z", 1), ("T", 1), ("S", 0), ("T", 2), ("S", 1), ("T", 3), ("F", 0), ("S", 2),
+    ("Z", 0), ("U", 0), ("Z", 1), ("U", 1), ("S", 0), ("T", 2), ("S", 1), ("T", 3), ("F", 0), ("S", 2),
     ("F", 1), ("S", 3), ("F", 2), ("F", 3),
 )
 X_OFFSETS = ((1, 0), (3, 0), (2, 0), (1, 1), (3, 1), (2, 1), (0, 1))
@@ -555,7 +555,10 @@
         y_pass(yb2.at[k], True)
         back_first_b(k)
 
-    steps = dict(Z=z_stage, T=back_both, S=inverse_two, F=inverse_one)
+    def early(h):
+        back_third(1, h)
+
+    steps = dict(U=early, Z=z_stage, T=back_both, S=inverse_two, F=inverse_one)
     for name, k in BACKWARD:
         steps[name](k)
     drain(o_ref, out_sem)

time: 185 us -> 187 us (1.011)
  no operation moved by 1% of the time
where the time goes in v4:
time: 187 us; the launch traced here: 186 us
  Pallas kernels  180 us (96%)
  local copies, waits for them, and re-layouts  6.47 us (3%)
    pallas_call x1, Pallas kernels, local(): pl.pallas_call(kernel, out_shape=jax.ShapeDtypeStruct((BZ, BX, BY), F32),...  180 us
    unnamed x7, local copies, waits for them, and re-layouts  6.47 us

profile of v4, /device:TPU:1, one launch (start us, length us, event | category | flops | bytes accessed | tf_op | source)
XLA Modules:
  0.0 186.4 jit_solution(3885561404279712664)
XLA Ops:
  0.0 0.0 copy-start
  0.0 2.2 %copy-done = f32[64,128,128]{2,1,0:T(8,128)S(1)} copy-done((f32[64,128,128]{2,1,0:T(8,128)S(1)}, f32[64,128,128]{2,1,0:T(8,128)}, u32[]{:S(2)}) %copy-start) | copy-done | bytes 4194328
  2.2 0.0 copy-start.1
  2.2 1.1 copy-done.1
  3.3 0.0 copy-start.2
  3.3 1.1 copy-done.2
  4.5 179.9 %shard_map.37 = f32[64,128,128]{2,1,0:T(8,128)S(1)} custom-call(f32[64,128,128]{2,1,0:T(8,128)S(1)} %copy-done, bf16[3,256,512]{2,1,0:T(8,128)(2,1)S(1)} %copy-done.2, bf16[3,512,256]{2,1,0:T(8,128)(2,1)S(1)} %copy-done.1), custom_call_target="tpu_custom_call" | custom-call | tf_op jit(solution)/shard_map/pallas_call | solution.py:580
  184.4 2.0 %copy.5 = f32[64,128,128]{2,1,0:T(8,128)} copy(f32[64,128,128]{2,1,0:T(8,128)S(1)} %shard_map.37) | data formatting | bytes 8388608
Async XLA Ops:
  0.0 2.2 %copy-start = (f32[64,128,128]{2,1,0:T(8,128)S(1)}, f32[64,128,128]{2,1,0:T(8,128)}, u32[]{:S(2)}) copy-start(f32[64,128,128]{2,1,0:T(8,128)} %c_ref.1) | copy-start | bytes 12582916
  2.2 1.1 copy-start.1
  3.3 1.1 copy-start.2
